TPU v7x, 256 devices: a whole 4x4x8 slice. The times are simulated.
256 devices in a mesh: wide: 64 (over z, x, core), narrow: 4 (over y).
Axes of the slice: x: 4, y: 4, z: 8, core: 2. Of those that a mesh axis runs over, the one named last changes fastest.
Arguments:
- query_states: bfloat16 [4096, 8192], P('wide', 'narrow'), may hold values from -8 to 8
- key_states: bfloat16 [4096, 8192], P('wide', 'narrow'), may hold values from -8 to 8
- value_states: bfloat16 [4096, 8192], P('wide', 'narrow'), may hold values from -6 to 6
- cache_keys: bfloat16 [4096, 1024], P('wide'), may hold values from -8 to 8
- cache_values: bfloat16 [4096, 1024], P('wide'), may hold values from -6 to 6
- gate_fast: bfloat16 [8, 512, 512], P('narrow'), may hold values from -0.25 to 0.25
- lift_fast: bfloat16 [8, 512, 512], P('narrow'), may hold values from -0.25 to 0.25
- down_fast: bfloat16 [8, 512, 512], P('narrow'), may hold values from -0.25 to 0.25
- token_rates: float32 [8, 8192], replicated, may hold values from 0.05 to 1
Outputs:
- attended: bfloat16 [4096, 8192], P('wide', 'narrow')
- recalled: bfloat16 [4096, 8192], P('wide', 'narrow')
All inputs are finite; a program needn't handle non-finite values.
Results may differ from a plain program's by a relative error of at most 0.0094.
Values may be sent and summed in bfloat16 or wider, within the bound.
A program may use at most 64 MiB of HBM per device.

v0:
```python
import functools
import math

import jax
import jax.numpy as jnp
from jax import lax
from jax.experimental import pallas as pl
from jax.experimental.pallas import tpu as pltpu
from jax.sharding import Mesh
from jax.sharding import PartitionSpec as P

WIDE = ("z", "x", "c")
EPS = 1e-06
COEF_A = 3.4445
COEF_B = -4.775
COEF_C = 2.0315
HALF = 1024
BLK = 256
NBLK = HALF // BLK
SCALE = math.log2(math.e) / math.sqrt(128)
F32 = jnp.float32
BF16 = jnp.bfloat16


def dot(a, b):
    return lax.dot_general(a, b, (((1,), (0,)), ((), ())), preferred_element_type=F32)


def dot_t(a, b):
    return lax.dot_general(a, b, (((1,), (1,)), ((), ())), preferred_element_type=F32)


def local(src, dst, sem):
    return pltpu.make_async_copy(src, dst, sem)


def remote(src, dst, send, recv, device):
    return pltpu.make_async_remote_copy(
        src_ref=src,
        dst_ref=dst,
        send_sem=send,
        recv_sem=recv,
        device_id=device,
        device_id_type=pl.DeviceIdType.MESH,
    )


def kernel(
    q_in, k_in, v_in, ck_in, cv_in, g_in, l_in, d_in, r_in,
    att, rec,
    kf, vf, kp, vp, qa, qf, wf, wd, wdt, kt, sc, ao, gd, gs, rr, yf, xs, zs, ls, fr, fd, ro, rt,
    s_loc, s_hp, s_qa, s_par, s_ring, s_fwd, s_wy, s_wp, s_wr, s_wf, s_wd, s_qf, s_rs, s_ag, s_ag2,
    s_agp, s_oa, s_or, snd,
):
    z = lax.axis_index("z")
    x = lax.axis_index("x")
    c = lax.axis_index("c")
    y = lax.axis_index("y")
    p = 1 - c
    right = lax.rem(x + 1, 4)
    left = lax.rem(x + 3, 4)
    far = lax.rem(x + 2, 4)
    onward = lax.rem(x + 1 + 2 * c, 4)
    behind = lax.rem(x + 3 + 2 * c, 4)
    me = 2 * x + c
    head = lax.rem(z, 2)
    home = z // 2
    source = y == home
    partner = (z, x, p, y)

    def rows(start, size):
        return pl.ds(pl.multiple_of(start, size), size)

    def cols(start, size):
        return pl.ds(pl.multiple_of(start, size), size)

    mine = rows(me * 64, 64)
    half = cols(c * HALF, HALF)
    other = cols(p * HALF, HALF)
    own = rows(c * 64, 64)

    loads = [
        local(k_in.at[:, half], kf.at[mine, :], s_loc.at[0]),
        local(v_in.at[:, half], vf.at[mine, :], s_loc.at[1]),
        local(q_in.at[:, cols(c * HALF + x * BLK, BLK)], qf.at[mine, :], s_loc.at[2]),
        local(r_in.at[:, cols(y * 2 * HALF + c * HALF, HALF)], rt, s_loc.at[3]),
    ]
    for load in loads:
        load.start()
    own_q = local(q_in.at[:, half], qa.at[own, :], s_qa.at[c])
    own_q.start()

    @pl.when(c == 1)
    def _():
        local(k_in.at[:, :HALF], kp.at[own, :], s_hp.at[0, c]).start()
        local(v_in.at[:, :HALF], vp.at[own, :], s_hp.at[1, c]).start()

    @pl.when((c == 0) & (y == 0))
    def _():
        local(ck_in, kp.at[own, :], s_hp.at[0, c]).start()
        local(cv_in, vp.at[own, :], s_hp.at[1, c]).start()

    full_weights = [
        local(g_in.at[head], wf.at[0], s_wy.at[0]),
        local(l_in.at[head], wf.at[1], s_wy.at[1]),
        local(d_in.at[head], wd, s_wy.at[2]),
    ]

    @pl.when(source)
    def _():
        for load in full_weights:
            load.start()

    barrier = pltpu.get_barrier_semaphore()
    peers = [partner]
    for step in range(1, 4):
        for core in range(2):
            peers.append((z, lax.rem(x + step, 4), core, y))
            peers.append((z, x, core, lax.rem(y + step, 4)))
    for peer in peers:
        pl.semaphore_signal(barrier, inc=1, device_id=peer, device_id_type=pl.DeviceIdType.MESH)
    pl.semaphore_wait(barrier, len(peers))

    gate_piece = rows(x * 128 + c * 64, 64)
    down_rows = rows(c * 256, 256)
    quarter = cols(x * 128, 128)

    @pl.when(source)
    def _():
        for step in range(1, 4):
            to = (z, x, c, lax.rem(y + step, 4))
            remote(
                g_in.at[head, gate_piece, :], wf.at[0, gate_piece, :], snd.at[0], s_wy.at[0], to
            ).start()
            remote(
                l_in.at[head, gate_piece, :], wf.at[1, gate_piece, :], snd.at[0], s_wy.at[1], to
            ).start()
            remote(
                d_in.at[head, down_rows, quarter],
                wd.at[down_rows, quarter],
                snd.at[0],
                s_wy.at[2],
                to,
            ).start()

    share = [
        remote(k_in.at[:, other], kf.at[mine, :], snd.at[1], s_par.at[0], partner),
        remote(v_in.at[:, other], vf.at[mine, :], snd.at[2], s_par.at[1], partner),
        remote(q_in.at[:, other], qa.at[own, :], snd.at[3], s_qa.at[c], partner),
    ]
    for copy in share:
        copy.start()

    def prior(ks, vs, to):
        return [
            remote(ks, kp.at[own, :], snd.at[4], s_hp.at[0, c], to),
            remote(vs, vp.at[own, :], snd.at[5], s_hp.at[1, c], to),
        ]

    within = prior(k_in.at[:, :HALF], v_in.at[:, :HALF], partner)
    cached = prior(ck_in, cv_in, partner)
    above = (z, x, 0, lax.rem(y + 1, 4))
    halo = [
        remote(k_in.at[:, HALF:], kp.at[own, :], snd.at[6], s_hp.at[0, c], above),
        remote(v_in.at[:, HALF:], vp.at[own, :], snd.at[7], s_hp.at[1, c], above),
    ]

    @pl.when(c == 0)
    def _():
        for copy in within:
            copy.start()

    @pl.when((c == 1) & (y == 0))
    def _():
        for copy in cached:
            copy.start()

    for block in range(NBLK):
        for index, (src, dst) in enumerate(((k_in, kf), (v_in, vf))):
            for way, to in enumerate((right, left)):
                for core in range(2):
                    remote(
                        src.at[:, core * HALF + block * BLK : core * HALF + (block + 1) * BLK],
                        dst.at[mine, block * BLK : (block + 1) * BLK],
                        snd.at[8 + index],
                        s_ring.at[index, block, way],
                        (z, to, core, y),
                    ).start()

    @pl.when(y < 3)
    def _():
        for copy in halo:
            copy.start()

    def ask(to_x, to_c):
        remote(
            q_in.at[:, cols(to_c * HALF + to_x * BLK, BLK)],
            qf.at[mine, :],
            snd.at[10],
            s_qf,
            (z, to_x, to_c, y),
        ).start()

    weight_share = [
        remote(wf.at[0, gate_piece, :], wf.at[0, gate_piece, :], snd.at[11], s_wp.at[0], partner),
        remote(wf.at[1, gate_piece, :], wf.at[1, gate_piece, :], snd.at[12], s_wp.at[1], partner),
        remote(
            wd.at[down_rows, quarter], wd.at[down_rows, quarter], snd.at[13], s_wp.at[2], partner
        ),
    ]
    arrivals = [
        remote(wf.at[0, gate_piece, :], wf.at[0, gate_piece, :], snd.at[11], s_wy.at[0], partner),
        remote(wf.at[1, gate_piece, :], wf.at[1, gate_piece, :], snd.at[12], s_wy.at[1], partner),
        remote(
            wd.at[down_rows, quarter], wd.at[down_rows, quarter], snd.at[13], s_wy.at[2], partner
        ),
    ]

    @pl.when(jnp.logical_not(source))
    def _():
        for copy, arrival in zip(weight_share, arrivals):
            arrival.wait_recv()
            copy.start()

    def onward_copy(index, dst, block):
        part = dst.at[rows(behind * 128, 128), block * BLK : (block + 1) * BLK]
        return remote(part, part, snd.at[14 + index], s_fwd.at[index, block], (z, onward, c, y))

    for block in range(NBLK):
        for index, dst in enumerate((kf, vf)):
            for way in range(2):
                part = dst.at[rows(behind * 128, 128), block * BLK : (block + 1) * BLK]
                remote(part, part, snd.at[14], s_ring.at[index, block, way], partner).wait_recv()
            onward_copy(index, dst, block).start()

    ask(x, p)
    for step in range(1, 4):
        for core in range(2):
            ask(lax.rem(x + step, 4), core)

    def piece_copies(chip, send, recv, to):
        gate = rows(chip * 128 + c * 64, 64)
        side = cols(chip * 128, 128)
        return [
            remote(wf.at[0, gate, :], wf.at[0, gate, :], send, recv, to),
            remote(wf.at[1, gate, :], wf.at[1, gate, :], send, recv, to),
            remote(wd.at[down_rows, side], wd.at[down_rows, side], send, recv, to),
        ]

    @pl.when(jnp.logical_not(source))
    def _():
        for way, to in enumerate((right, left)):
            for copy in piece_copies(x, snd.at[16], s_wr.at[way], (z, to, c, y)):
                copy.start()

    for load in loads:
        load.wait()
    own_q.wait()
    theirs = qa.at[rows(p * 64, 64), :]
    remote(theirs, theirs, snd.at[3], s_qa.at[p], partner).wait_recv()
    for index, dst in enumerate((kp, vp)):
        for core in range(2):
            part = dst.at[core * 64 : (core + 1) * 64, :]
            remote(part, part, snd.at[4], s_hp.at[index, core], partner).wait_recv()
    for index, dst in enumerate((kf, vf)):
        part = dst.at[rows((2 * x + p) * 64, 64), :]
        remote(part, part, snd.at[1], s_par.at[index], partner).wait_recv()

    chip = rows(x * 128, 128)
    for block in range(NBLK):
        span = slice(block * BLK, (block + 1) * BLK)
        kt[block * BLK : (block + 1) * BLK, :] = kp[:, span].T
        kt[HALF + block * BLK : HALF + (block + 1) * BLK, :] = kf[chip, span].T

    row_at = lax.broadcasted_iota(jnp.int32, (BLK, BLK), 0)
    col_at = lax.broadcasted_iota(jnp.int32, (BLK, BLK), 1)

    def attend(block):
        first = block * BLK
        asked = qa[:, first : first + BLK]
        top = jnp.full((1, BLK), -jnp.inf, F32)
        for part in range(5):
            at = first + part * BLK
            scores = dot(kt[at : at + BLK, :], asked) * SCALE
            if part == 0:
                scores = jnp.where(row_at > col_at, scores, -jnp.inf)
            if part == 4:
                scores = jnp.where(row_at <= col_at, scores, -jnp.inf)
            sc[part * BLK : (part + 1) * BLK, :] = scores
            top = jnp.maximum(top, jnp.max(scores, axis=0, keepdims=True))
        total = jnp.zeros((1, BLK), F32)
        blend = jnp.zeros((128, BLK), F32)
        for part in range(5):
            at = first + part * BLK
            raised = jnp.exp2(sc[part * BLK : (part + 1) * BLK, :] - top)
            total = total + jnp.sum(raised, axis=0, keepdims=True)
            if at < HALF:
                held = vp[:, at : at + BLK]
            else:
                held = vf[chip, at - HALF : at - HALF + BLK]
            blend = blend + dot(held, raised.astype(BF16))
        ao[:, first : first + BLK] = (blend / total).astype(BF16)

    attend(0)
    attend(1)

    @pl.when(source)
    def _():
        for load in full_weights:
            load.wait()

    @pl.when(jnp.logical_not(source))
    def _():
        theirs = rows(x * 128 + p * 64, 64)
        across = wd.at[rows(p * 256, 256), quarter]
        for index in range(2):
            part = wf.at[index, theirs, :]
            remote(part, part, snd.at[11], s_wp.at[index], partner).wait_recv()
        remote(across, across, snd.at[13], s_wp.at[2], partner).wait_recv()

    for block in range(4):
        wdt[:, block * 128 : (block + 1) * 128] = wd[block * 128 : (block + 1) * 128, quarter].T

    gd[...] = jnp.zeros_like(gd)
    for block in range(NBLK):
        span = slice(block * BLK, (block + 1) * BLK)
        for index, dst in enumerate((kf, vf)):
            part = dst.at[rows(far * 128, 128), span]
            remote(part, part, snd.at[14], s_fwd.at[index, block], partner).wait_recv()
        keys = kf[:, span]
        rate = rt[pl.ds(z, 1), span]
        target = (-(vf[:, span].astype(F32) * rate)).astype(BF16)
        pre_gate = dot(wf[0, chip, :], keys)
        pre_lift = dot(wf[1, chip, :], keys)
        back = dot(wdt[...], target)
        sig = 1.0 / (1.0 + jnp.exp(-pre_gate))
        silu = pre_gate * sig
        hidden = (silu * pre_lift).astype(BF16)
        back_lift = (back * silu).astype(BF16)
        back_gate = (back * pre_lift * sig * (1.0 + pre_gate * (1.0 - sig))).astype(BF16)
        gd[0:128, :] += dot_t(back_gate, keys)
        gd[128:256, :] += dot_t(back_lift, keys)
        gd[256:384, :] += dot_t(hidden, target)

    me_y = 2 * y + c

    for owner in range(8):
        for index in range(3):
            at = index * 128 + owner * 16
            gs[owner, index] = gd[at : at + 16, :].astype(BF16)
    for step in range(1, 8):
        owner = lax.rem(me_y + step, 8)
        remote(
            gs.at[owner], rr.at[me_y], snd.at[17], s_rs, (z, x, lax.rem(owner, 2), owner // 2)
        ).start()
    attend(2)
    remote(rr.at[0:7], rr.at[0:7], snd.at[17], s_rs, partner).wait_recv()
    place = 4 * x + y
    for index in range(3):
        whole = gd[rows(index * 128 + me_y * 16, 16), :]
        for step in range(1, 8):
            whole = whole + rr[lax.rem(me_y + step, 8), index].astype(F32)
        yf[index, place, c] = whole.astype(BF16)

    piece = yf.at[:, place, c]
    for step in range(1, 4):
        remote(piece, piece, snd.at[18], s_ag.at[0, step], (z, x, c, lax.rem(y + step, 4))).start()
        remote(piece, piece, snd.at[18], s_ag.at[1, step], (z, lax.rem(x + step, 4), c, y)).start()
    remote(piece, piece, snd.at[19], s_agp, partner).start()
    for step in range(1, 4):
        at_y = 4 * x + lax.rem(y + 4 - step, 4)
        part = yf.at[:, at_y, c]
        remote(part, part, snd.at[18], s_ag.at[0, step], partner).wait_recv()
        side = yf.at[:, at_y, c, :, 0:256]
        for hop in range(1, 4):
            remote(side, side, snd.at[20], s_ag2, (z, lax.rem(x + hop, 4), c, y)).start()
        remote(part, part, snd.at[19], s_agp, partner).start()
        at_x = 4 * lax.rem(x + 4 - step, 4) + y
        part = yf.at[:, at_x, c]
        remote(part, part, snd.at[18], s_ag.at[1, step], partner).wait_recv()
        side = yf.at[:, at_x, c, :, 256:512]
        for hop in range(1, 4):
            remote(side, side, snd.at[20], s_ag2, (z, x, c, lax.rem(y + hop, 4))).start()
        remote(part, part, snd.at[19], s_agp, partner).start()

    @pl.when(jnp.logical_not(source))
    def _():
        bytes_of = wf.at[0, 0:192, :]
        for way in range(2):
            remote(bytes_of, bytes_of, snd.at[16], s_wr.at[way], partner).wait_recv()
        for copy in piece_copies(behind, snd.at[21], s_wf, (z, onward, c, y)):
            copy.start()
        for side in (right, left):
            for copy in piece_copies(side, snd.at[22], s_wd, partner):
                copy.start()

    attend(3)
    local(ao.at[own, :], att.at[:, half], s_loc.at[4]).start()
    give = remote(ao.at[rows(p * 64, 64), :], att.at[:, half], snd.at[23], s_oa, partner)
    give.start()

    @pl.when(jnp.logical_not(source))
    def _():
        bytes_of = wf.at[0, 0:192, :]
        remote(bytes_of, bytes_of, snd.at[21], s_wf, partner).wait_recv()
        for copy in piece_copies(far, snd.at[22], s_wd, partner):
            copy.start()

    crossed = yf.at[:, 0:9, 0]
    remote(crossed, crossed, snd.at[20], s_ag2, partner).wait_recv()
    for step in range(1, 4):
        for hop in range(1, 4):
            part = yf.at[:, 4 * lax.rem(x + step, 4) + lax.rem(y + hop, 4), c]
            remote(part, part, snd.at[19], s_agp, partner).start()
    remote(yf.at[:, :, 0], yf.at[:, :, 0], snd.at[19], s_agp, partner).wait_recv()

    def ortho(index, carry):
        rounded = yf[index].reshape(512, 512).astype(F32)
        norm = jnp.sqrt(jnp.sum(jnp.square(rounded), keepdims=True) + EPS)
        xs[index] = (rounded / norm).astype(BF16)
        for _ in range(2):
            zs[...] = dot_t(xs[index], xs[index]).astype(BF16)
            ls[...] = dot(zs[...], xs[index]).astype(BF16)
            xs[index] = (
                COEF_A * xs[index].astype(F32)
                + COEF_B * ls[...].astype(F32)
                + COEF_C * dot(zs[...], ls[...])
            ).astype(BF16)
        return carry

    lax.fori_loop(0, 3, ortho, 0)

    @pl.when(jnp.logical_not(source))
    def _():
        bytes_of = kf.at[0:288, :]
        remote(bytes_of, bytes_of, snd.at[22], s_wd, partner).wait_recv()

    def fresh(weight, turned):
        initial = weight.astype(F32)
        moved = initial - turned.astype(F32)
        wanted = jnp.sqrt(jnp.mean(jnp.square(initial), axis=-1, keepdims=True) + EPS)
        present = jnp.sqrt(jnp.mean(jnp.square(moved), axis=-1, keepdims=True) + EPS)
        return (moved * (wanted / present)).astype(BF16)

    for index in range(2):
        fr[index] = fresh(wf[index], xs[index])
    fd[...] = fresh(wd[...], xs[2].T)

    remote(qf.at[0:448, :], qf.at[0:448, :], snd.at[10], s_qf, partner).wait_recv()
    query_gate = dot(fr[0], qf[...])
    query_lift = dot(fr[1], qf[...])
    query_hidden = (query_gate / (1.0 + jnp.exp(-query_gate)) * query_lift).astype(BF16)
    ro[...] = dot(fd[...], query_hidden).astype(BF16)
    tokens = cols(c * HALF + x * BLK, BLK)

    def answer(to_x, to_c):
        remote(
            ro.at[rows((2 * to_x + to_c) * 64, 64), :],
            rec.at[:, tokens],
            snd.at[24],
            s_or,
            (z, to_x, to_c, y),
        ).start()

    for step in (2, 1, 3):
        for core in range(2):
            answer(lax.rem(x + step, 4), core)
    answer(x, p)
    local(ro.at[mine, :], rec.at[:, tokens], s_loc.at[5]).start()

    local(ao.at[own, :], att.at[:, half], s_loc.at[4]).wait()
    local(ro.at[mine, :], rec.at[:, tokens], s_loc.at[5]).wait()
    give.wait_send()
    remote(ao.at[own, :], att.at[:, other], snd.at[23], s_oa, partner).wait_recv()
    for copy in share:
        copy.wait_send()

    @pl.when(c == 0)
    def _():
        for copy in within:
            copy.wait_send()

    @pl.when((c == 1) & (y == 0))
    def _():
        for copy in cached:
            copy.wait_send()

    @pl.when(y < 3)
    def _():
        for copy in halo:
            copy.wait_send()

    def drain(ref, index):
        remote(ref, ref, snd.at[index], s_or, partner).wait_send()

    @pl.when(source)
    def _():
        drain(kf.at[0:288, :], 0)

    for index in range(2):
        drain(kf.at[0:256, :], 8 + index)
        drain(kf.at[0:128, :], 14 + index)
    drain(qf.at[0:448, :], 10)

    @pl.when(jnp.logical_not(source))
    def _():
        for copy in weight_share:
            copy.wait_send()
        drain(wf.at[0, 0:384, :], 16)
        drain(wf.at[0, 0:192, :], 21)
        drain(kf.at[0:288, :], 22)

    drain(rr.at[0:7], 17)
    drain(yf.at[:, 0:6, 0], 18)
    drain(yf.at[:, :, 0], 19)
    drain(yf.at[:, 0:9, 0], 20)
    drain(qf.at[0:448, :], 24)
    remote(qf.at[0:448, :], qf.at[0:448, :], snd.at[24], s_or, partner).wait_recv()


def per_device(*arrays):
    any_spec = pl.BlockSpec(memory_space=pl.ANY)
    out = jax.ShapeDtypeStruct((64, 2 * HALF), BF16)
    vmem = pltpu.VMEM
    dma = pltpu.SemaphoreType.DMA
    return pl.pallas_call(
        kernel,
        out_shape=(out, out),
        in_specs=[any_spec] * 9,
        out_specs=(any_spec, any_spec),
        scratch_shapes=[
            vmem((512, HALF), BF16),
            vmem((512, HALF), BF16),
            vmem((128, HALF), BF16),
            vmem((128, HALF), BF16),
            vmem((128, HALF), BF16),
            vmem((512, BLK), BF16),
            vmem((2, 512, 512), BF16),
            vmem((512, 512), BF16),
            vmem((128, 512), BF16),
            vmem((2 * HALF, 128), BF16),
            vmem((5 * BLK, BLK), F32),
            vmem((128, HALF), BF16),
            vmem((384, 512), F32),
            vmem((8, 3, 16, 512), BF16),
            vmem((8, 3, 16, 512), BF16),
            vmem((3, 16, 2, 16, 512), BF16),
            vmem((3, 512, 512), BF16),
            vmem((512, 512), BF16),
            vmem((512, 512), BF16),
            vmem((2, 512, 512), BF16),
            vmem((512, 512), BF16),
            vmem((512, BLK), BF16),
            vmem((8, HALF), F32),
            dma((6,)),
            dma((2, 2)),
            dma((2,)),
            dma((2,)),
            dma((2, NBLK, 2)),
            dma((2, NBLK)),
            dma((3,)),
            dma((3,)),
            dma((2,)),
            dma(()),
            dma(()),
            dma(()),
            dma(()),
            dma((2, 4)),
            dma(()),
            dma(()),
            dma(()),
            dma(()),
            dma((25,)),
        ],
        compiler_params=pltpu.CompilerParams(
            collective_id=0, has_side_effects=True, vmem_limit_bytes=48 * 1024 * 1024
        ),
        name="plane",
    )(*arrays)


def solution(mesh):
    split = Mesh(mesh.devices.reshape(8, 4, 2, 4), ("z", "x", "c", "y"))
    tokens = P(WIDE, "y")
    heads = P("y", None, None)
    return jax.shard_map(
        per_device,
        mesh=split,
        in_specs=(tokens, tokens, tokens, P(WIDE), P(WIDE), heads, heads, heads, P()),
        out_specs=(tokens, tokens),
        check_vma=False,
    )
```

profile of v0, /device:TPU:1, one launch (start us, length us, event | category | flops | bytes accessed | tf_op | source)
XLA Modules:
  0.0 73.8 jit_solution(7779228553958901079)
XLA Ops:
  0.6 0.0 copy-start
  0.6 1.2 %copy-done = bf16[2,512,512]{2,1,0:T(8,128)(2,1)S(1)} copy-done((bf16[2,512,512]{2,1,0:T(8,128)(2,1)S(1)}, bf16[2,512,512]{2,1,0:T(8,128)(2,1)}, u32[]{:S(2)}) %copy-start) | copy-done | bytes 1048600
  1.9 0.0 copy-start.1
  1.9 1.2 %copy-done.1 = bf16[2,512,512]{2,1,0:T(8,128)(2,1)S(1)} copy-done((bf16[2,512,512]{2,1,0:T(8,128)(2,1)S(1)}, bf16[2,512,512]{2,1,0:T(8,128)(2,1)}, u32[]{:S(2)}) %copy-start.1) | copy-done | bytes 1048600
  3.1 0.0 copy-start.2
  3.1 1.2 %copy-done.2 = bf16[2,512,512]{2,1,0:T(8,128)(2,1)S(1)} copy-done((bf16[2,512,512]{2,1,0:T(8,128)(2,1)S(1)}, bf16[2,512,512]{2,1,0:T(8,128)(2,1)}, u32[]{:S(2)}) %copy-start.2) | copy-done | bytes 1048600
  4.3 0.0 copy-start.3
  4.3 0.9 %copy-done.3 = bf16[64,2048]{1,0:T(8,128)(2,1)S(1)} copy-done((bf16[64,2048]{1,0:T(8,128)(2,1)S(1)}, bf16[64,2048]{1,0:T(8,128)(2,1)}, u32[]{:S(2)}) %copy-start.3) | copy-done | bytes 262168
  5.3 0.0 copy-start.4
  5.3 0.9 %copy-done.4 = bf16[64,2048]{1,0:T(8,128)(2,1)S(1)} copy-done((bf16[64,2048]{1,0:T(8,128)(2,1)S(1)}, bf16[64,2048]{1,0:T(8,128)(2,1)}, u32[]{:S(2)}) %copy-start.4) | copy-done | bytes 262168
  6.2 0.0 copy-start.5
  6.2 0.9 %copy-done.5 = bf16[64,2048]{1,0:T(8,128)(2,1)S(1)} copy-done((bf16[64,2048]{1,0:T(8,128)(2,1)S(1)}, bf16[64,2048]{1,0:T(8,128)(2,1)}, u32[]{:S(2)}) %copy-start.5) | copy-done | bytes 262168
  7.2 0.0 copy-start.6
  7.2 0.9 %copy-done.6 = f32[8,8192]{1,0:T(8,128)S(1)} copy-done((f32[8,8192]{1,0:T(8,128)S(1)}, f32[8,8192]{1,0:T(8,128)}, u32[]{:S(2)}) %copy-start.6) | copy-done | bytes 262168
  8.1 0.0 copy-start.7
  8.1 0.9 %copy-done.7 = bf16[64,1024]{1,0:T(8,128)(2,1)S(1)} copy-done((bf16[64,1024]{1,0:T(8,128)(2,1)S(1)}, bf16[64,1024]{1,0:T(8,128)(2,1)}, u32[]{:S(2)}) %copy-start.7) | copy-done | bytes 131096
  9.0 0.0 copy-start.8
  9.0 0.9 %copy-done.8 = bf16[64,1024]{1,0:T(8,128)(2,1)S(1)} copy-done((bf16[64,1024]{1,0:T(8,128)(2,1)S(1)}, bf16[64,1024]{1,0:T(8,128)(2,1)}, u32[]{:S(2)}) %copy-start.8) | copy-done | bytes 131096
  9.9 62.5 %plane.1 = (bf16[64,2048]{1,0:T(8,128)(2,1)S(1)}, bf16[64,2048]{1,0:T(8,128)(2,1)S(1)}) custom-call(bf16[64,2048]{1,0:T(8,128)(2,1)S(1)} %copy-done.3, bf16[64,2048]{1,0:T(8,128)(2,1)S(1)} %copy-done.4, bf16[64,2048]{1,0:T(8,128)(2,1)S(1)} %copy-done.5, bf16[64,1024]{1,0:T(8,128)(2,1)S(1)} %copy-done.7, bf16[64,1024]{1,0:T(8,128)(2,1)S(1)} %copy-done.8, ...), custom_call_target="tpu_custom_call" | custom-call | tf_op jit(solution)/shard_map/plane/pallas_call | solution.py:526
  72.4 0.7 copy.13
  73.1 0.7 copy.14
Async XLA Ops:
  0.6 1.2 %copy-start = (bf16[2,512,512]{2,1,0:T(8,128)(2,1)S(1)}, bf16[2,512,512]{2,1,0:T(8,128)(2,1)}, u32[]{:S(2)}) copy-start(bf16[2,512,512]{2,1,0:T(8,128)(2,1)} %g_in.1) | copy-start | bytes 3145732
  1.9 1.2 %copy-start.1 = (bf16[2,512,512]{2,1,0:T(8,128)(2,1)S(1)}, bf16[2,512,512]{2,1,0:T(8,128)(2,1)}, u32[]{:S(2)}) copy-start(bf16[2,512,512]{2,1,0:T(8,128)(2,1)} %l_in.1) | copy-start | bytes 3145732
  3.1 1.2 %copy-start.2 = (bf16[2,512,512]{2,1,0:T(8,128)(2,1)S(1)}, bf16[2,512,512]{2,1,0:T(8,128)(2,1)}, u32[]{:S(2)}) copy-start(bf16[2,512,512]{2,1,0:T(8,128)(2,1)} %d_in.1) | copy-start | bytes 3145732
  4.3 0.9 %copy-start.3 = (bf16[64,2048]{1,0:T(8,128)(2,1)S(1)}, bf16[64,2048]{1,0:T(8,128)(2,1)}, u32[]{:S(2)}) copy-start(bf16[64,2048]{1,0:T(8,128)(2,1)} %q_in.1) | copy-start | bytes 786436
  5.3 0.9 %copy-start.4 = (bf16[64,2048]{1,0:T(8,128)(2,1)S(1)}, bf16[64,2048]{1,0:T(8,128)(2,1)}, u32[]{:S(2)}) copy-start(bf16[64,2048]{1,0:T(8,128)(2,1)} %k_in.1) | copy-start | bytes 786436
  6.2 0.9 %copy-start.5 = (bf16[64,2048]{1,0:T(8,128)(2,1)S(1)}, bf16[64,2048]{1,0:T(8,128)(2,1)}, u32[]{:S(2)}) copy-start(bf16[64,2048]{1,0:T(8,128)(2,1)} %v_in.1) | copy-start | bytes 786436
  7.2 0.9 %copy-start.6 = (f32[8,8192]{1,0:T(8,128)S(1)}, f32[8,8192]{1,0:T(8,128)}, u32[]{:S(2)}) copy-start(f32[8,8192]{1,0:T(8,128)} %r_in.1) | copy-start | bytes 786436
  8.1 0.9 %copy-start.7 = (bf16[64,1024]{1,0:T(8,128)(2,1)S(1)}, bf16[64,1024]{1,0:T(8,128)(2,1)}, u32[]{:S(2)}) copy-start(bf16[64,1024]{1,0:T(8,128)(2,1)} %ck_in.1) | copy-start | bytes 393220
  9.0 0.9 %copy-start.8 = (bf16[64,1024]{1,0:T(8,128)(2,1)S(1)}, bf16[64,1024]{1,0:T(8,128)(2,1)}, u32[]{:S(2)}) copy-start(bf16[64,1024]{1,0:T(8,128)(2,1)} %cv_in.1) | copy-start | bytes 393220
where the time goes:
time: 74.8 us; the launch traced here: 73.8 us
  Pallas kernels  62.5 us (84%)
  local copies, waits for them, and re-layouts  10.7 us (14%)
    pallas_call x1, Pallas kernels, per_device(): pl.pallas_call(kernel, out_shape=(out, out), in_specs=[any_spec] * 9, out...  62.5 us
    unnamed x20, local copies, waits for them, and re-layouts  10.7 us

commit v1 on v0

v1 whole, which is shorter than its diff:
```python
import functools
import math

import jax
import jax.numpy as jnp
from jax import lax
from jax.experimental import pallas as pl
from jax.experimental.pallas import tpu as pltpu
from jax.sharding import Mesh
from jax.sharding import PartitionSpec as P

WIDE = ("z", "x", "c")
EPS = 1e-06
COEF_A = 3.4445
COEF_B = -4.775
COEF_C = 2.0315
HALF = 1024
BLK = 256
NBLK = HALF // BLK
SCALE = math.log2(math.e) / math.sqrt(128)
F32 = jnp.float32
BF16 = jnp.bfloat16


def dot(a, b):
    return lax.dot_general(a, b, (((1,), (0,)), ((), ())), preferred_element_type=F32)


def dot_t(a, b):
    return lax.dot_general(a, b, (((1,), (1,)), ((), ())), preferred_element_type=F32)


def local(src, dst, sem):
    return pltpu.make_async_copy(src, dst, sem)


def remote(src, dst, send, recv, device):
    return pltpu.make_async_remote_copy(
        src_ref=src,
        dst_ref=dst,
        send_sem=send,
        recv_sem=recv,
        device_id=device,
        device_id_type=pl.DeviceIdType.MESH,
    )


def kernel(
    q_in, k_in, v_in, ck_in, cv_in, g_in, l_in, d_in, r_in,
    att, rec,
    kf, vf, qf, kp, vp, wm, wq, wdq, wdr, wdt, kt, sc, ao, gd, ps, pr, gs, rr, ym, yd, xs, zs, ls,
    fr, fd, ro, rt,
    s_loc, s_hp, s_par, s_ring, s_fwd, s_wy, s_wp, s_wr, s_wf, s_qr, s_qfw, s_rsp, s_rs, s_ag, s_ag2,
    s_dag, s_dag2, s_dp, s_fr, s_oa, s_or, snd,
):
    z = lax.axis_index("z")
    x = lax.axis_index("x")
    c = lax.axis_index("c")
    y = lax.axis_index("y")
    p = 1 - c
    right = lax.rem(x + 1, 4)
    left = lax.rem(x + 3, 4)
    far = lax.rem(x + 2, 4)
    onward = lax.rem(x + 1 + 2 * c, 4)
    behind = lax.rem(x + 3 + 2 * c, 4)
    me = 2 * x + c
    head = lax.rem(z, 2)
    source = y == z // 2
    partner = (z, x, p, y)

    def at(start, size):
        return pl.ds(pl.multiple_of(start, size), size)

    mine = at(me * 64, 64)
    half = at(c * HALF, HALF)
    other = at(p * HALF, HALF)
    own = at(c * 64, 64)
    theirs = at(p * 64, 64)
    quarter = at(x * 128, 128)
    down_rows = at(c * 256, 256)
    down_piece = at(x * 128 + c * 64, 64)

    def got(ref, sem):
        remote(ref, ref, snd.at[0], sem, partner).wait_recv()

    loads = [
        local(k_in.at[:, half], kf.at[mine, :], s_loc.at[0]),
        local(v_in.at[:, half], vf.at[mine, :], s_loc.at[1]),
        local(q_in.at[:, half], qf.at[mine, :], s_loc.at[2]),
        local(r_in.at[:, at(y * 2 * HALF + c * HALF, HALF)], rt, s_loc.at[3]),
    ]
    for load in loads:
        load.start()

    @pl.when(c == 1)
    def _():
        local(k_in.at[:, :HALF], kp.at[own, :], s_hp.at[0, c]).start()
        local(v_in.at[:, :HALF], vp.at[own, :], s_hp.at[1, c]).start()

    @pl.when((c == 0) & (y == 0))
    def _():
        local(ck_in, kp.at[own, :], s_hp.at[0, c]).start()
        local(cv_in, vp.at[own, :], s_hp.at[1, c]).start()

    def full_weights(first, second):
        return [
            local(first.at[head], wm, s_wy.at[0]),
            local(second.at[head, quarter, :], wq.at[at(p * 128, 128), :], s_wy.at[1]),
            local(d_in.at[head, :, quarter], wdq, s_wy.at[2]),
            local(d_in.at[head, quarter, :], wdr, s_wy.at[3]),
        ]

    for core, (first, second) in enumerate(((g_in, l_in), (l_in, g_in))):

        @pl.when(source & (c == core))
        def _():
            for load in full_weights(first, second):
                load.start()

    barrier = pltpu.get_barrier_semaphore()
    peers = [partner]
    for step in range(1, 4):
        for core in range(2):
            peers.append((z, lax.rem(x + step, 4), core, y))
            peers.append((z, x, core, lax.rem(y + step, 4)))
    for peer in peers:
        pl.semaphore_signal(barrier, inc=1, device_id=peer, device_id_type=pl.DeviceIdType.MESH)
    pl.semaphore_wait(barrier, len(peers))

    for core, first in enumerate((g_in, l_in)):

        @pl.when(source & (c == core))
        def _():
            for step in (2, 1, 3):
                to = (z, x, c, lax.rem(y + step, 4))
                remote(
                    first.at[head, quarter, :], wm.at[quarter, :], snd.at[0], s_wy.at[0], to
                ).start()
                remote(
                    d_in.at[head, down_rows, quarter],
                    wdq.at[down_rows, :],
                    snd.at[0],
                    s_wy.at[1],
                    to,
                ).start()

    share = [
        remote(k_in.at[:, other], kf.at[mine, :], snd.at[1], s_par.at[0], partner),
        remote(v_in.at[:, other], vf.at[mine, :], snd.at[2], s_par.at[1], partner),
        remote(q_in.at[:, other], qf.at[mine, :], snd.at[3], s_par.at[2], partner),
    ]
    for copy in share:
        copy.start()

    def prior(ks, vs, to, index):
        return [
            remote(ks, kp.at[own, :], snd.at[index], s_hp.at[0, c], to),
            remote(vs, vp.at[own, :], snd.at[index + 1], s_hp.at[1, c], to),
        ]

    within = prior(k_in.at[:, :HALF], v_in.at[:, :HALF], partner, 4)
    cached = prior(ck_in, cv_in, partner, 4)
    halo = prior(k_in.at[:, HALF:], v_in.at[:, HALF:], (z, x, 0, lax.rem(y + 1, 4)), 25)

    @pl.when(c == 0)
    def _():
        for copy in within:
            copy.start()

    @pl.when((c == 1) & (y == 0))
    def _():
        for copy in cached:
            copy.start()

    def spread(src, dst, send, recv, first, size):
        for way, to in enumerate((right, left)):
            for core in range(2):
                remote(
                    src.at[:, core * HALF + first : core * HALF + first + size],
                    dst.at[mine, first : first + size],
                    send,
                    recv.at[way],
                    (z, to, core, y),
                ).start()

    for block in range(NBLK):
        for index, (src, dst) in enumerate(((k_in, kf), (v_in, vf))):
            spread(src, dst, snd.at[8 + index], s_ring.at[index, block], block * BLK, BLK)

    @pl.when(y < 3)
    def _():
        for copy in halo:
            copy.start()

    @pl.when(source)
    def _():
        for step in (2, 1, 3):
            to = (z, x, c, lax.rem(y + step, 4))
            remote(
                d_in.at[head, down_piece, :], wdr.at[own, :], snd.at[6], s_wy.at[2], to
            ).start()

    for block in range(NBLK):
        span = slice(block * BLK, (block + 1) * BLK)
        for index, dst in enumerate((kf, vf)):
            part = dst.at[at(behind * 128, 128), span]
            for way in range(2):
                got(part, s_ring.at[index, block, way])
            remote(part, part, snd.at[14], s_fwd.at[index, block], (z, onward, c, y)).start()

    spread(q_in, qf, snd.at[10], s_qr, 0, HALF)

    wm_quarter = wm.at[quarter, :]
    weight_share = [
        remote(wm_quarter, wq.at[at(c * 128, 128), :], snd.at[11], s_wp.at[0], partner),
        remote(wdq.at[down_rows, :], wdq.at[down_rows, :], snd.at[12], s_wp.at[1], partner),
    ]

    @pl.when(jnp.logical_not(source))
    def _():
        got(wm_quarter, s_wy.at[0])
        got(wdq.at[down_rows, :], s_wy.at[1])
        for copy in weight_share:
            copy.start()
        for way, to in enumerate((right, left)):
            remote(wm_quarter, wm_quarter, snd.at[16], s_wr.at[way], (z, to, c, y)).start()

    for load in loads:
        load.wait()
    for index, dst in enumerate((kp, vp)):
        for core in range(2):
            got(dst.at[core * 64 : (core + 1) * 64, :], s_hp.at[index, core])
    for index, dst in enumerate((kf, vf, qf)):
        got(dst.at[at((2 * x + p) * 64, 64), :], s_par.at[index])

    for block in range(NBLK):
        span = slice(block * BLK, (block + 1) * BLK)
        kt[block * BLK : (block + 1) * BLK, :] = kp[:, span].T
        kt[HALF + block * BLK : HALF + (block + 1) * BLK, :] = kf[quarter, span].T

    row_at = lax.broadcasted_iota(jnp.int32, (BLK, BLK), 0)
    col_at = lax.broadcasted_iota(jnp.int32, (BLK, BLK), 1)

    def attend(block):
        first = block * BLK
        asked = qf[quarter, first : first + BLK]
        top = jnp.full((1, BLK), -jnp.inf, F32)
        for part in range(5):
            key = first + part * BLK
            scores = dot(kt[key : key + BLK, :], asked) * SCALE
            if part == 0:
                scores = jnp.where(row_at > col_at, scores, -jnp.inf)
            if part == 4:
                scores = jnp.where(row_at <= col_at, scores, -jnp.inf)
            sc[part * BLK : (part + 1) * BLK, :] = scores
            top = jnp.maximum(top, jnp.max(scores, axis=0, keepdims=True))
        total = jnp.zeros((1, BLK), F32)
        blend = jnp.zeros((128, BLK), F32)
        for part in range(5):
            key = first + part * BLK
            raised = jnp.exp2(sc[part * BLK : (part + 1) * BLK, :] - top)
            total = total + jnp.sum(raised, axis=0, keepdims=True)
            if key < HALF:
                held = vp[:, key : key + BLK]
            else:
                held = vf[quarter, key - HALF : key - HALF + BLK]
            blend = blend + dot(held, raised.astype(BF16))
        ao[:, first : first + BLK] = (blend / total).astype(BF16)

    attend(0)

    for core, (first, second) in enumerate(((g_in, l_in), (l_in, g_in))):

        @pl.when(source & (c == core))
        def _():
            for load in full_weights(first, second):
                load.wait()

    @pl.when(jnp.logical_not(source))
    def _():
        got(wq.at[at(p * 128, 128), :], s_wp.at[0])
        got(wdq.at[at(p * 256, 256), :], s_wp.at[1])

    wq[at(c * 128, 128), :] = wm[quarter, :]
    for block in range(4):
        wdt[:, block * 128 : (block + 1) * 128] = wdq[block * 128 : (block + 1) * 128, :].T

    gd[...] = jnp.zeros_like(gd)
    for block in range(NBLK):
        span = slice(block * BLK, (block + 1) * BLK)
        for index, dst in enumerate((kf, vf)):
            got(dst.at[at(far * 128, 128), span], s_fwd.at[index, block])
        keys = kf[:, span]
        rate = rt[pl.ds(z, 1), span]
        target = (-(vf[:, span].astype(F32) * rate)).astype(BF16)
        pre_gate = dot(wq[0:128, :], keys)
        pre_lift = dot(wq[128:256, :], keys)
        back = dot(wdt[...], target)
        sig = 1.0 / (1.0 + jnp.exp(-pre_gate))
        silu = pre_gate * sig
        hidden = (silu * pre_lift).astype(BF16)
        back_lift = (back * silu).astype(BF16)
        back_gate = (back * pre_lift * sig * (1.0 + pre_gate * (1.0 - sig))).astype(BF16)
        gd[0:128, :] += dot_t(back_gate, keys)
        gd[128:256, :] += dot_t(back_lift, keys)
        gd[256:384, :] += dot_t(hidden, target)

    ps[0:128, :] = gd[at(p * 128, 128), :].astype(BF16)
    ps[128:192, :] = gd[at(256 + p * 64, 64), :].astype(BF16)
    remote(ps, pr, snd.at[15], s_rsp, partner).start()
    attend(1)
    got(pr, s_rsp)
    for owner in range(4):
        main = gd[at(c * 128 + owner * 32, 32), :] + pr[owner * 32 : owner * 32 + 32, :].astype(F32)
        down = (
            gd[at(256 + c * 64 + owner * 16, 16), :]
            + pr[128 + owner * 16 : 144 + owner * 16, :].astype(F32)
        )
        gs[owner, 0:32, :] = main.astype(BF16)
        gs[owner, 32:48, :] = down.astype(BF16)
        ls[owner * 48 : owner * 48 + 32, :] = main
        ls[owner * 48 + 32 : owner * 48 + 48, :] = down
    for step in (2, 1, 3):
        owner = lax.rem(y + step, 4)
        remote(gs.at[owner], rr.at[y], snd.at[17], s_rs, (z, x, c, owner)).start()
    attend(2)
    attend(3)
    local(ao.at[own, :], att.at[:, half], s_loc.at[4]).start()
    give = remote(ao.at[theirs, :], att.at[:, half], snd.at[23], s_oa, partner)
    give.start()
    got(rr.at[0:3], s_rs)
    whole = ls[at(y * 48, 48), :]
    for step in range(1, 4):
        whole = whole + rr[lax.rem(y + step, 4)].astype(F32)
    place = 4 * x + y
    ym[place] = whole[0:32].astype(BF16)
    mark_d = 4 * (2 * x + c) + y
    yd[mark_d] = whole[32:48].astype(BF16)

    def gather(ref, index_of, first, second, send):
        own_piece = index_of(x, y)
        low, high = slice(0, 256), slice(256, 512)

        def put(index, span, recv, to):
            part = ref.at[index, :, span]
            remote(part, part, send, recv, to).start()

        for step in (2, 1, 3):
            put(own_piece, low, first.at[0, step], (z, x, c, lax.rem(y + step, 4)))
            put(own_piece, high, first.at[1, step], (z, lax.rem(x + step, 4), c, y))
        for step in (2, 1, 3):
            put(own_piece, low, second, (z, lax.rem(x + step, 4), c, y))
            put(own_piece, high, second, (z, x, c, lax.rem(y + step, 4)))

    def relay(ref, index_of, first, second, send):
        low, high = slice(0, 256), slice(256, 512)
        for step in (1, 3, 2):
            across = index_of(x, lax.rem(y + 4 - step, 4))
            part = ref.at[across, :, low]
            got(part, first.at[0, step])
            for hop in (2, 1, 3):
                to = (z, lax.rem(x + hop, 4), c, y)
                remote(part, part, send, second, to).start()
            along = index_of(lax.rem(x + 4 - step, 4), y)
            part = ref.at[along, :, high]
            got(part, first.at[1, step])
            for hop in (2, 1, 3):
                to = (z, x, c, lax.rem(y + hop, 4))
                remote(part, part, send, second, to).start()

    def main_at(xx, yy):
        return 4 * xx + yy

    def down_at(xx, yy):
        return 4 * (2 * xx + c) + yy

    gather(ym, main_at, s_ag, s_ag2, snd.at[18])
    gather(yd, down_at, s_dag, s_dag2, snd.at[19])
    relay(ym, main_at, s_ag, s_ag2, snd.at[18])
    relay(yd, down_at, s_dag, s_dag2, snd.at[19])

    @pl.when(jnp.logical_not(source))
    def _():
        for way in range(2):
            got(wm_quarter, s_wr.at[way])
        part = wm.at[at(behind * 128, 128), :]
        remote(part, part, snd.at[21], s_wf, (z, onward, c, y)).start()
        got(wdr.at[own, :], s_wy.at[2])
        remote(wdr.at[own, :], wdr.at[own, :], snd.at[22], s_wp.at[2], partner).start()

    for way in range(2):
        got(qf.at[at(behind * 128, 128), :], s_qr.at[way])
    part = qf.at[at(behind * 128, 128), :]
    remote(part, part, snd.at[7], s_qfw, (z, onward, c, y)).start()

    def begin(rounded):
        wide = rounded.astype(F32)
        norm = jnp.sqrt(jnp.sum(jnp.square(wide), keepdims=True) + EPS)
        return (wide / norm).astype(BF16)

    def sweep():
        zs[...] = dot_t(xs[...], xs[...]).astype(BF16)
        fd[...] = dot(zs[...], xs[...]).astype(BF16)
        xs[...] = (
            COEF_A * xs[...].astype(F32)
            + COEF_B * fd[...].astype(F32)
            + COEF_C * dot(zs[...], fd[...])
        ).astype(BF16)

    def fresh(weight, turned):
        initial = weight.astype(F32)
        moved = initial - turned.astype(F32)
        wanted = jnp.sqrt(jnp.mean(jnp.square(initial), axis=-1, keepdims=True) + EPS)
        present = jnp.sqrt(jnp.mean(jnp.square(moved), axis=-1, keepdims=True) + EPS)
        return (moved * (wanted / present)).astype(BF16)

    got(ym.at[0:12], s_ag2)
    xs[...] = begin(ym[...].reshape(512, 512))
    sweep()
    sweep()

    got(yd.at[0:12], s_dag2)
    halves = [yd.at[at(8 * chip + 4 * c, 4)] for chip in range(4)]
    for chip in range(4):
        remote(halves[chip], halves[chip], snd.at[20], s_dp, partner).start()

    @pl.when(jnp.logical_not(source))
    def _():
        got(wm.at[at(far * 128, 128), :], s_wf)

    fr[c] = fresh(wm[...], xs[...])
    lend = remote(fr.at[c], fr.at[c], snd.at[13], s_fr, partner)
    lend.start()

    got(yd.at[0:16], s_dp)
    xs[...] = begin(yd[...].reshape(512, 512))
    sweep()
    zs[...] = dot_t(xs[...], xs[...]).astype(BF16)
    side = xs[:, quarter]
    lifted = dot(zs[...], side).astype(BF16)
    turned = (
        COEF_A * side.astype(F32) + COEF_B * lifted.astype(F32) + COEF_C * dot(zs[...], lifted)
    ).astype(BF16)

    @pl.when(jnp.logical_not(source))
    def _():
        got(wdr.at[theirs, :], s_wp.at[2])

    wdt[...] = fresh(wdr[...], turned.T)

    got(qf.at[at(far * 128, 128), :], s_qfw)
    got(fr.at[p], s_fr)
    for block in range(NBLK):
        span = slice(block * BLK, (block + 1) * BLK)
        asked = qf[:, span]
        query_gate = dot(fr[0], asked)
        query_lift = dot(fr[1], asked)
        query_hidden = (query_gate / (1.0 + jnp.exp(-query_gate)) * query_lift).astype(BF16)
        ro[:, span] = dot(wdt[...], query_hidden).astype(BF16)
        here = at(c * HALF + block * BLK, BLK)
        remote(ro.at[theirs, span], rec.at[:, here], snd.at[24], s_or, partner).start()
        local(ro.at[own, span], rec.at[:, here], s_loc.at[5 + block]).start()

    def drain(ref, index):
        remote(ref, ref, snd.at[index], s_or, partner).wait_send()

    for block in range(NBLK):
        span = slice(block * BLK, (block + 1) * BLK)
        local(ro.at[own, span], ro.at[own, span], s_loc.at[5 + block]).wait()
    local(ao.at[own, :], att.at[:, half], s_loc.at[4]).wait()
    give.wait_send()
    got(ao.at[own, :], s_oa)
    lend.wait_send()
    for copy in share:
        copy.wait_send()

    @pl.when(c == 0)
    def _():
        for copy in within:
            copy.wait_send()

    @pl.when((c == 1) & (y == 0))
    def _():
        for copy in cached:
            copy.wait_send()

    @pl.when(y < 3)
    def _():
        for copy in halo:
            copy.wait_send()

    @pl.when(source)
    def _():
        drain(kf.at[0:288, :], 0)
        drain(wm.at[0:192, :], 6)

    for index in range(2):
        drain(kf.at[0:256, :], 8 + index)
    drain(kf.at[0:256, :], 14)
    drain(kf.at[0:256, :], 10)
    drain(kf.at[0:128, :], 7)

    @pl.when(jnp.logical_not(source))
    def _():
        for copy in weight_share:
            copy.wait_send()
        drain(wm.at[0:256, :], 16)
        drain(wm.at[0:128, :], 21)
        drain(wdr.at[own, :], 22)

    drain(pr, 15)
    drain(rr.at[0:3], 17)
    drain(ym.at[0:15], 18)
    drain(yd.at[0:15], 19)
    drain(yd.at[0:16], 20)
    drain(ro.at[0:64, :], 24)
    got(ro.at[0:64, :], s_or)


def per_device(*arrays):
    any_spec = pl.BlockSpec(memory_space=pl.ANY)
    out = jax.ShapeDtypeStruct((64, 2 * HALF), BF16)
    vmem = pltpu.VMEM
    dma = pltpu.SemaphoreType.DMA
    return pl.pallas_call(
        kernel,
        out_shape=(out, out),
        in_specs=[any_spec] * 9,
        out_specs=(any_spec, any_spec),
        scratch_shapes=[
            vmem((512, HALF), BF16),
            vmem((512, HALF), BF16),
            vmem((512, HALF), BF16),
            vmem((128, HALF), BF16),
            vmem((128, HALF), BF16),
            vmem((512, 512), BF16),
            vmem((256, 512), BF16),
            vmem((512, 128), BF16),
            vmem((128, 512), BF16),
            vmem((128, 512), BF16),
            vmem((2 * HALF, 128), BF16),
            vmem((5 * BLK, BLK), F32),
            vmem((128, HALF), BF16),
            vmem((384, 512), F32),
            vmem((192, 512), BF16),
            vmem((192, 512), BF16),
            vmem((4, 48, 512), BF16),
            vmem((4, 48, 512), BF16),
            vmem((16, 32, 512), BF16),
            vmem((32, 16, 512), BF16),
            vmem((512, 512), BF16),
            vmem((512, 512), BF16),
            vmem((192, 512), F32),
            vmem((2, 512, 512), BF16),
            vmem((512, 512), BF16),
            vmem((128, HALF), BF16),
            vmem((8, HALF), F32),
            dma((9,)),
            dma((2, 2)),
            dma((3,)),
            dma((2, NBLK, 2)),
            dma((2, NBLK)),
            dma((4,)),
            dma((3,)),
            dma((2,)),
            dma(()),
            dma((2,)),
            dma(()),
            dma(()),
            dma(()),
            dma((2, 4)),
            dma(()),
            dma((2, 4)),
            dma(()),
            dma(()),
            dma(()),
            dma(()),
            dma(()),
            dma((27,)),
        ],
        compiler_params=pltpu.CompilerParams(
            collective_id=0, has_side_effects=True, vmem_limit_bytes=67000000
        ),
        name="plane",
    )(*arrays)


def solution(mesh):
    split = Mesh(mesh.devices.reshape(8, 4, 2, 4), ("z", "x", "c", "y"))
    tokens = P(WIDE, "y")
    heads = P("y", None, None)
    return jax.shard_map(
        per_device,
        mesh=split,
        in_specs=(tokens, tokens, tokens, P(WIDE), P(WIDE), heads, heads, heads, P()),
        out_specs=(tokens, tokens),
        check_vma=False,
    )
```

time: 74.8 us -> 56.6 us (0.76); the launches traced: 73.8 us -> 56.5 us
  Pallas kernels: 62.5 us -> 53.4 us
  local copies, waits for them, and re-layouts: 10.7 us -> 2.42 us
    pallas_call x1, Pallas kernels: 62.5 us -> 53.4 us  [per_device(): pl.pallas_call(kernel, out_shape=(out, out), in_specs=[any_spec] * 9, out...]
    unnamed x20 -> x4, local copies, waits for them, and re-layouts: 10.7 us -> 2.42 us
where the time goes in v1:
time: 56.6 us; the launch traced here: 56.5 us
  Pallas kernels  53.4 us (94%)
  local copies, waits for them, and re-layouts  2.42 us (4%)
  between operations  0.65 us (1%)
    pallas_call x1, Pallas kernels, per_device(): pl.pallas_call(kernel, out_shape=(out, out), in_specs=[any_spec] * 9, out...  53.4 us
    unnamed x4, local copies, waits for them, and re-layouts  2.42 us

profile of v1, /device:TPU:1, one launch (start us, length us, event | category | flops | bytes accessed | tf_op | source)
XLA Modules:
  0.0 56.5 jit_solution(15163745917159678173)
XLA Ops:
  0.6 53.4 %plane.1 = (bf16[64,2048]{1,0:T(8,128)(2,1)}, bf16[64,2048]{1,0:T(8,128)(2,1)}) custom-call(bf16[64,2048]{1,0:T(8,128)(2,1)} %q_in.1, bf16[64,2048]{1,0:T(8,128)(2,1)} %k_in.1, bf16[64,2048]{1,0:T(8,128)(2,1)} %v_in.1, bf16[64,1024]{1,0:T(8,128)(2,1)} %ck_in.1, bf16[64,1024]{1,0:T(8,128)(2,1)} %cv_in.1, bf16[2,512,512]{2,1,0:T(8,128)(2,1)} %g_in.1, ...), custom_call_target="tpu_custom_call" | custom-call | tf_op jit(solution)/shard_map/plane/pallas_call | solution.py:525
  54.1 0.0 copy-start
  54.1 1.7 %copy.13 = bf16[64,2048]{1,0:T(8,128)(2,1)} copy(bf16[64,2048]{1,0:T(8,128)(2,1)} %get-tuple-element.4) | data formatting | bytes 524288
  55.8 0.0 copy-done
  55.8 0.7 %copy.14 = bf16[64,2048]{1,0:T(8,128)(2,1)} copy(bf16[64,2048]{1,0:T(8,128)(2,1)S(1)} %copy-done) | data formatting | bytes 524288
Async XLA Ops:
  54.1 1.7 %copy-start = (bf16[64,2048]{1,0:T(8,128)(2,1)S(1)}, bf16[64,2048]{1,0:T(8,128)(2,1)}, u32[]{:S(2)}) copy-start(bf16[64,2048]{1,0:T(8,128)(2,1)} %get-tuple-element.5) | copy-start | bytes 786436

commit v2 on v1

--- a/solution.py
+++ b/solution.py
@@ -61,8 +61,6 @@
     right = lax.rem(x + 1, 4)
     left = lax.rem(x + 3, 4)
     far = lax.rem(x + 2, 4)
-    onward = lax.rem(x + 1 + 2 * c, 4)
-    behind = lax.rem(x + 3 + 2 * c, 4)
     me = 2 * x + c
     head = lax.rem(z, 2)
     source = y == z // 2
@@ -200,15 +198,14 @@
                 d_in.at[head, down_piece, :], wdr.at[own, :], snd.at[6], s_wy.at[2], to
             ).start()
 
+    chips = (left, right)
     for block in range(NBLK):
         span = slice(block * BLK, (block + 1) * BLK)
         for index, dst in enumerate((kf, vf)):
-            part = dst.at[at(behind * 128, 128), span]
-            for way in range(2):
-                got(part, s_ring.at[index, block, way])
-            remote(part, part, snd.at[14], s_fwd.at[index, block], (z, onward, c, y)).start()
-
-    spread(q_in, qf, snd.at[10], s_qr, 0, HALF)
+            part = dst.at[at(chips[index] * 128, 128), span]
+            got(part, s_ring.at[index, block, index])
+            to = (z, chips[1 - index], c, y)
+            remote(part, part, snd.at[14], s_fwd.at[index, block], to).start()
 
     wm_quarter = wm.at[quarter, :]
     weight_share = [
@@ -224,6 +221,8 @@
             copy.start()
         for way, to in enumerate((right, left)):
             remote(wm_quarter, wm_quarter, snd.at[16], s_wr.at[way], (z, to, c, y)).start()
+
+    spread(q_in, qf, snd.at[10], s_qr, 0, HALF)
 
     for load in loads:
         load.wait()
@@ -289,6 +288,7 @@
     for block in range(NBLK):
         span = slice(block * BLK, (block + 1) * BLK)
         for index, dst in enumerate((kf, vf)):
+            got(dst.at[at(chips[1 - index] * 128, 128), span], s_ring.at[index, block, 1 - index])
             got(dst.at[at(far * 128, 128), span], s_fwd.at[index, block])
         keys = kf[:, span]
         rate = rt[pl.ds(z, 1), span]
@@ -305,52 +305,64 @@
         gd[128:256, :] += dot_t(back_lift, keys)
         gd[256:384, :] += dot_t(hidden, target)
 
-    ps[0:128, :] = gd[at(p * 128, 128), :].astype(BF16)
-    ps[128:192, :] = gd[at(256 + p * 64, 64), :].astype(BF16)
-    remote(ps, pr, snd.at[15], s_rsp, partner).start()
+    main, down = slice(0, 128), slice(128, 192)
+    ps[main, :] = gd[at(p * 128, 128), :].astype(BF16)
+    remote(ps.at[main, :], pr.at[main, :], snd.at[15], s_rsp.at[0], partner).start()
+    ps[down, :] = gd[at(256 + p * 64, 64), :].astype(BF16)
+    remote(ps.at[down, :], pr.at[down, :], snd.at[28], s_rsp.at[1], partner).start()
     attend(1)
-    got(pr, s_rsp)
-    for owner in range(4):
-        main = gd[at(c * 128 + owner * 32, 32), :] + pr[owner * 32 : owner * 32 + 32, :].astype(F32)
-        down = (
-            gd[at(256 + c * 64 + owner * 16, 16), :]
-            + pr[128 + owner * 16 : 144 + owner * 16, :].astype(F32)
-        )
-        gs[owner, 0:32, :] = main.astype(BF16)
-        gs[owner, 32:48, :] = down.astype(BF16)
-        ls[owner * 48 : owner * 48 + 32, :] = main
-        ls[owner * 48 + 32 : owner * 48 + 48, :] = down
-    for step in (2, 1, 3):
-        owner = lax.rem(y + step, 4)
-        remote(gs.at[owner], rr.at[y], snd.at[17], s_rs, (z, x, c, owner)).start()
+
+    def pair_and_send(index, span, first, size, low):
+        got(pr.at[span, :], s_rsp.at[index])
+        rows = slice(low, low + size)
+        for owner in range(4):
+            begin_at = span.start + owner * size
+            both = gd[at(first + owner * size, size), :] + pr[
+                begin_at : begin_at + size, :
+            ].astype(F32)
+            gs[owner, rows, :] = both.astype(BF16)
+            ls[begin_at : begin_at + size, :] = both
+        for step in (2, 1, 3):
+            owner = lax.rem(y + step, 4)
+            remote(
+                gs.at[owner, rows, :],
+                rr.at[y, rows, :],
+                snd.at[17 + 10 * index],
+                s_rs.at[index],
+                (z, x, c, owner),
+            ).start()
+
+    def summed(index, span, size, low):
+        rows = slice(low, low + size)
+        got(rr.at[0:3, rows, :], s_rs.at[index])
+        whole = ls[at(span.start + y * size, size), :]
+        for step in range(1, 4):
+            whole = whole + rr[lax.rem(y + step, 4), rows, :].astype(F32)
+        return whole.astype(BF16)
+
+    pair_and_send(0, main, c * 128, 32, 0)
+    pair_and_send(1, down, 256 + c * 64, 16, 32)
     attend(2)
     attend(3)
     local(ao.at[own, :], att.at[:, half], s_loc.at[4]).start()
     give = remote(ao.at[theirs, :], att.at[:, half], snd.at[23], s_oa, partner)
     give.start()
-    got(rr.at[0:3], s_rs)
-    whole = ls[at(y * 48, 48), :]
-    for step in range(1, 4):
-        whole = whole + rr[lax.rem(y + step, 4)].astype(F32)
-    place = 4 * x + y
-    ym[place] = whole[0:32].astype(BF16)
-    mark_d = 4 * (2 * x + c) + y
-    yd[mark_d] = whole[32:48].astype(BF16)
-
-    def gather(ref, index_of, first, second, send):
-        own_piece = index_of(x, y)
-        low, high = slice(0, 256), slice(256, 512)
-
-        def put(index, span, recv, to):
-            part = ref.at[index, :, span]
-            remote(part, part, send, recv, to).start()
-
+    ym[4 * x + y] = summed(0, main, 32, 0)
+
+    def gather(ref, index, ways, recv_low, recv_high, send):
         for step in (2, 1, 3):
-            put(own_piece, low, first.at[0, step], (z, x, c, lax.rem(y + step, 4)))
-            put(own_piece, high, first.at[1, step], (z, lax.rem(x + step, 4), c, y))
-        for step in (2, 1, 3):
-            put(own_piece, low, second, (z, lax.rem(x + step, 4), c, y))
-            put(own_piece, high, second, (z, x, c, lax.rem(y + step, 4)))
+            in_y = (z, x, c, lax.rem(y + step, 4))
+            in_x = (z, lax.rem(x + step, 4), c, y)
+            low, high = ref.at[index, :, 0:256], ref.at[index, :, 256:512]
+            to_low, to_high = (in_y, in_x) if ways == 0 else (in_x, in_y)
+            remote(low, low, send, recv_low(step), to_low).start()
+            remote(high, high, send, recv_high(step), to_high).start()
+
+    def gather_first(ref, index, first, send):
+        gather(ref, index, 0, lambda n: first.at[0, n], lambda n: first.at[1, n], send)
+
+    def gather_rest(ref, index, second, send):
+        gather(ref, index, 1, lambda n: second, lambda n: second, send)
 
     def relay(ref, index_of, first, second, send):
         low, high = slice(0, 256), slice(256, 512)
@@ -374,24 +386,30 @@
     def down_at(xx, yy):
         return 4 * (2 * xx + c) + yy
 
-    gather(ym, main_at, s_ag, s_ag2, snd.at[18])
-    gather(yd, down_at, s_dag, s_dag2, snd.at[19])
+    gather_first(ym, main_at(x, y), s_ag, snd.at[18])
+    gather_rest(ym, main_at(x, y), s_ag2, snd.at[18])
+    yd[down_at(x, y)] = summed(1, down, 16, 32)
+    gather_first(yd, down_at(x, y), s_dag, snd.at[19])
     relay(ym, main_at, s_ag, s_ag2, snd.at[18])
+    gather_rest(yd, down_at(x, y), s_dag2, snd.at[19])
     relay(yd, down_at, s_dag, s_dag2, snd.at[19])
 
     @pl.when(jnp.logical_not(source))
     def _():
         for way in range(2):
             got(wm_quarter, s_wr.at[way])
-        part = wm.at[at(behind * 128, 128), :]
-        remote(part, part, snd.at[21], s_wf, (z, onward, c, y)).start()
+        for index in range(2):
+            part = wm.at[at(chips[index] * 128 + index * 64, 64), :]
+            to = (z, chips[1 - index], c, y)
+            remote(part, part, snd.at[21], s_wf.at[index], to).start()
         got(wdr.at[own, :], s_wy.at[2])
         remote(wdr.at[own, :], wdr.at[own, :], snd.at[22], s_wp.at[2], partner).start()
 
     for way in range(2):
-        got(qf.at[at(behind * 128, 128), :], s_qr.at[way])
-    part = qf.at[at(behind * 128, 128), :]
-    remote(part, part, snd.at[7], s_qfw, (z, onward, c, y)).start()
+        got(qf.at[at(chips[way] * 128, 128), :], s_qr.at[way])
+        part = qf.at[at(chips[way] * 128, 128), way * 512 : way * 512 + 512]
+        to = (z, chips[1 - way], c, y)
+        remote(part, part, snd.at[7], s_qfw.at[way], to).start()
 
     def begin(rounded):
         wide = rounded.astype(F32)
@@ -426,7 +444,8 @@
 
     @pl.when(jnp.logical_not(source))
     def _():
-        got(wm.at[at(far * 128, 128), :], s_wf)
+        for index in range(2):
+            got(wm.at[at(far * 128 + index * 64, 64), :], s_wf.at[index])
 
     fr[c] = fresh(wm[...], xs[...])
     lend = remote(fr.at[c], fr.at[c], snd.at[13], s_fr, partner)
@@ -448,7 +467,8 @@
 
     wdt[...] = fresh(wdr[...], turned.T)
 
-    got(qf.at[at(far * 128, 128), :], s_qfw)
+    for way in range(2):
+        got(qf.at[at(far * 128, 128), way * 512 : way * 512 + 512], s_qfw.at[way])
     got(fr.at[p], s_fr)
     for block in range(NBLK):
         span = slice(block * BLK, (block + 1) * BLK)
@@ -508,8 +528,10 @@
         drain(wm.at[0:128, :], 21)
         drain(wdr.at[own, :], 22)
 
-    drain(pr, 15)
-    drain(rr.at[0:3], 17)
+    drain(pr.at[main, :], 15)
+    drain(pr.at[down, :], 28)
+    drain(rr.at[0:3, 0:32], 17)
+    drain(rr.at[0:3, 32:48], 27)
     drain(ym.at[0:15], 18)
     drain(yd.at[0:15], 19)
     drain(yd.at[0:16], 20)
@@ -517,12 +539,21 @@
     got(ro.at[0:64, :], s_or)
 
 
+def write_out(att, rec, att_out, rec_out, sem):
+    copies = [local(att, att_out, sem.at[0]), local(rec, rec_out, sem.at[1])]
+    for copy in copies:
+        copy.start()
+    for copy in copies:
+        copy.wait()
+
+
 def per_device(*arrays):
     any_spec = pl.BlockSpec(memory_space=pl.ANY)
-    out = jax.ShapeDtypeStruct((64, 2 * HALF), BF16)
+    out = pltpu.VMEM((64, 2 * HALF), BF16)
+    arrays = [pltpu.with_memory_space_constraint(a, pltpu.HBM) for a in arrays]
     vmem = pltpu.VMEM
     dma = pltpu.SemaphoreType.DMA
-    return pl.pallas_call(
+    held = pl.pallas_call(
         kernel,
         out_shape=(out, out),
         in_specs=[any_spec] * 9,
@@ -563,11 +594,11 @@
             dma((4,)),
             dma((3,)),
             dma((2,)),
-            dma(()),
             dma((2,)),
-            dma(()),
-            dma(()),
-            dma(()),
+            dma((2,)),
+            dma((2,)),
+            dma((2,)),
+            dma((2,)),
             dma((2, 4)),
             dma(()),
             dma((2, 4)),
@@ -576,13 +607,21 @@
             dma(()),
             dma(()),
             dma(()),
-            dma((27,)),
+            dma((29,)),
         ],
         compiler_params=pltpu.CompilerParams(
-            collective_id=0, has_side_effects=True, vmem_limit_bytes=67000000
+            collective_id=0, has_side_effects=True, vmem_limit_bytes=48000000
         ),
         name="plane",
     )(*arrays)
+    return pl.pallas_call(
+        write_out,
+        out_shape=(pltpu.HBM((64, 2 * HALF), BF16),) * 2,
+        in_specs=[pl.BlockSpec(memory_space=vmem)] * 2,
+        out_specs=(pl.BlockSpec(memory_space=pltpu.HBM),) * 2,
+        scratch_shapes=[dma((2,))],
+        name="write_out",
+    )(*[pltpu.with_memory_space_constraint(a, pltpu.VMEM) for a in held])
 
 
 def solution(mesh):

time: 56.6 us -> 52.8 us (0.933)
  local copies, waits for them, and re-layouts: 2.42 us -> 0 us
  Pallas kernels: 53.4 us -> 52.1 us
    unnamed x4 -> x0, local copies, waits for them, and re-layouts: 2.42 us -> none
    pallas_call x1, Pallas kernels: 53.4 us -> 51.3 us  [per_device(): pl.pallas_call(kernel, out_shape=(out, out), in_specs=[any_spec] * 9, out...]
    pallas_call x0 -> x1, Pallas kernels: none -> 0.81 us  [per_device(): pl.pallas_call(write_out, out_shape=(pltpu.HBM((64, 2 * HALF), BF16),) *...]
where the time goes in v2:
time: 52.8 us
  Pallas kernels  52.1 us (99%)
  between operations  0.64 us (1%)
    pallas_call x1, Pallas kernels, per_device(): pl.pallas_call(kernel, out_shape=(out, out), in_specs=[any_spec] * 9, out...  51.3 us

profile of v2, /device:TPU:1, one launch (start us, length us, event | category | flops | bytes accessed | tf_op | source)
XLA Modules:
  0.0 52.8 jit_solution(8955299642671518540)
XLA Ops:
  0.6 51.3 %plane.1 = (bf16[64,2048]{1,0:T(8,128)(2,1)S(1)}, bf16[64,2048]{1,0:T(8,128)(2,1)S(1)}) custom-call(bf16[64,2048]{1,0:T(8,128)(2,1)} %q_in.1, bf16[64,2048]{1,0:T(8,128)(2,1)} %k_in.1, bf16[64,2048]{1,0:T(8,128)(2,1)} %v_in.1, bf16[64,1024]{1,0:T(8,128)(2,1)} %ck_in.1, bf16[64,1024]{1,0:T(8,128)(2,1)} %cv_in.1, bf16[2,512,512]{2,1,0:T(8,128)(2,1)} %g_in.1, ...), custom_call_target="tpu_custom_call" | custom-call | tf_op jit(solution)/shard_map/plane/pallas_call | solution.py:556
  51.9 0.8 %write_out.1 = (bf16[64,2048]{1,0:T(8,128)(2,1)}, bf16[64,2048]{1,0:T(8,128)(2,1)}) custom-call(bf16[64,2048]{1,0:T(8,128)(2,1)S(1)} %get-tuple-element.4.att, bf16[64,2048]{1,0:T(8,128)(2,1)S(1)} %get-tuple-element.5.rec), custom_call_target="tpu_custom_call" | custom-call | tf_op jit(solution)/shard_map/write_out/pallas_call | solution.py:617

commit v3 on v2

--- a/solution.py
+++ b/solution.py
@@ -49,7 +49,7 @@
     q_in, k_in, v_in, ck_in, cv_in, g_in, l_in, d_in, r_in,
     att, rec,
     kf, vf, qf, kp, vp, wm, wq, wdq, wdr, wdt, kt, sc, ao, gd, ps, pr, gs, rr, ym, yd, xs, zs, ls,
-    fr, fd, ro, rt,
+    fr, fd, ro, rt, hq,
     s_loc, s_hp, s_par, s_ring, s_fwd, s_wy, s_wp, s_wr, s_wf, s_qr, s_qfw, s_rsp, s_rs, s_ag, s_ag2,
     s_dag, s_dag2, s_dp, s_fr, s_oa, s_or, snd,
 ):
@@ -305,11 +305,15 @@
         gd[128:256, :] += dot_t(back_lift, keys)
         gd[256:384, :] += dot_t(hidden, target)
 
-    main, down = slice(0, 128), slice(128, 192)
+    main, down = slice(0, 128), slice(128, 256)
     ps[main, :] = gd[at(p * 128, 128), :].astype(BF16)
     remote(ps.at[main, :], pr.at[main, :], snd.at[15], s_rsp.at[0], partner).start()
-    ps[down, :] = gd[at(256 + p * 64, 64), :].astype(BF16)
-    remote(ps.at[down, :], pr.at[down, :], snd.at[28], s_rsp.at[1], partner).start()
+
+    @pl.when(c == 0)
+    def _():
+        ps[down, :] = gd[256:384, :].astype(BF16)
+        remote(ps.at[down, :], pr.at[down, :], snd.at[28], s_rsp.at[1], partner).start()
+
     attend(1)
 
     def pair_and_send(index, span, first, size, low):
@@ -341,7 +345,11 @@
         return whole.astype(BF16)
 
     pair_and_send(0, main, c * 128, 32, 0)
-    pair_and_send(1, down, 256 + c * 64, 16, 32)
+
+    @pl.when(c == 1)
+    def _():
+        pair_and_send(1, down, 256, 32, 32)
+
     attend(2)
     attend(3)
     local(ao.at[own, :], att.at[:, half], s_loc.at[4]).start()
@@ -383,16 +391,21 @@
     def main_at(xx, yy):
         return 4 * xx + yy
 
-    def down_at(xx, yy):
-        return 4 * (2 * xx + c) + yy
-
-    gather_first(ym, main_at(x, y), s_ag, snd.at[18])
-    gather_rest(ym, main_at(x, y), s_ag2, snd.at[18])
-    yd[down_at(x, y)] = summed(1, down, 16, 32)
-    gather_first(yd, down_at(x, y), s_dag, snd.at[19])
+    place = main_at(x, y)
+    gather_first(ym, place, s_ag, snd.at[18])
+    gather_rest(ym, place, s_ag2, snd.at[18])
+
+    @pl.when(c == 1)
+    def _():
+        yd[place] = summed(1, down, 32, 32)
+        gather_first(yd, place, s_dag, snd.at[19])
+
     relay(ym, main_at, s_ag, s_ag2, snd.at[18])
-    gather_rest(yd, down_at(x, y), s_dag2, snd.at[19])
-    relay(yd, down_at, s_dag, s_dag2, snd.at[19])
+
+    @pl.when(c == 1)
+    def _():
+        gather_rest(yd, place, s_dag2, snd.at[19])
+        relay(yd, main_at, s_dag, s_dag2, snd.at[19])
 
     @pl.when(jnp.logical_not(source))
     def _():
@@ -406,10 +419,10 @@
         remote(wdr.at[own, :], wdr.at[own, :], snd.at[22], s_wp.at[2], partner).start()
 
     for way in range(2):
-        got(qf.at[at(chips[way] * 128, 128), :], s_qr.at[way])
-        part = qf.at[at(chips[way] * 128, 128), way * 512 : way * 512 + 512]
-        to = (z, chips[1 - way], c, y)
-        remote(part, part, snd.at[7], s_qfw.at[way], to).start()
+        rows = at(chips[way] * 128, 128)
+        got(qf.at[rows, :], s_qr.at[way])
+        part = qf.at[rows, way * 512 : way * 512 + 512]
+        remote(part, part, snd.at[7], s_qfw.at[way], (z, chips[1 - way], c, y)).start()
 
     def begin(rounded):
         wide = rounded.astype(F32)
@@ -437,11 +450,6 @@
     sweep()
     sweep()
 
-    got(yd.at[0:12], s_dag2)
-    halves = [yd.at[at(8 * chip + 4 * c, 4)] for chip in range(4)]
-    for chip in range(4):
-        remote(halves[chip], halves[chip], snd.at[20], s_dp, partner).start()
-
     @pl.when(jnp.logical_not(source))
     def _():
         for index in range(2):
@@ -451,35 +459,58 @@
     lend = remote(fr.at[c], fr.at[c], snd.at[13], s_fr, partner)
     lend.start()
 
-    got(yd.at[0:16], s_dp)
-    xs[...] = begin(yd[...].reshape(512, 512))
-    sweep()
-    zs[...] = dot_t(xs[...], xs[...]).astype(BF16)
-    side = xs[:, quarter]
-    lifted = dot(zs[...], side).astype(BF16)
-    turned = (
-        COEF_A * side.astype(F32) + COEF_B * lifted.astype(F32) + COEF_C * dot(zs[...], lifted)
-    ).astype(BF16)
-
     @pl.when(jnp.logical_not(source))
     def _():
         got(wdr.at[theirs, :], s_wp.at[2])
 
-    wdt[...] = fresh(wdr[...], turned.T)
+    lend_down = remote(fd.at[0:128, :], wdt, snd.at[20], s_dp, partner)
+
+    @pl.when(c == 1)
+    def _():
+        got(yd.at[0:12], s_dag2)
+        xs[...] = begin(yd[...].reshape(512, 512))
+        sweep()
+        zs[...] = dot_t(xs[...], xs[...]).astype(BF16)
+        side = xs[:, quarter]
+        lifted = dot(zs[...], side).astype(BF16)
+        turned = (
+            COEF_A * side.astype(F32) + COEF_B * lifted.astype(F32) + COEF_C * dot(zs[...], lifted)
+        ).astype(BF16)
+        new = fresh(wdr[...], turned.T)
+        fd[0:128, :] = new
+        wdt[...] = new
+        lend_down.start()
 
     for way in range(2):
         got(qf.at[at(far * 128, 128), way * 512 : way * 512 + 512], s_qfw.at[way])
     got(fr.at[p], s_fr)
-    for block in range(NBLK):
+
+    def hide(block):
         span = slice(block * BLK, (block + 1) * BLK)
         asked = qf[:, span]
         query_gate = dot(fr[0], asked)
         query_lift = dot(fr[1], asked)
-        query_hidden = (query_gate / (1.0 + jnp.exp(-query_gate)) * query_lift).astype(BF16)
-        ro[:, span] = dot(wdt[...], query_hidden).astype(BF16)
+        return (query_gate / (1.0 + jnp.exp(-query_gate)) * query_lift).astype(BF16)
+
+    def settle(block, hidden):
+        span = slice(block * BLK, (block + 1) * BLK)
+        ro[:, span] = dot(wdt[...], hidden).astype(BF16)
         here = at(c * HALF + block * BLK, BLK)
         remote(ro.at[theirs, span], rec.at[:, here], snd.at[24], s_or, partner).start()
         local(ro.at[own, span], rec.at[:, here], s_loc.at[5 + block]).start()
+
+    @pl.when(c == 0)
+    def _():
+        for block in range(NBLK):
+            hq[:, block * BLK : (block + 1) * BLK] = hide(block)
+        got(wdt, s_dp)
+        for block in range(NBLK):
+            settle(block, hq[:, block * BLK : (block + 1) * BLK])
+
+    @pl.when(c == 1)
+    def _():
+        for block in range(NBLK):
+            settle(block, hide(block))
 
     def drain(ref, index):
         remote(ref, ref, snd.at[index], s_or, partner).wait_send()
@@ -529,12 +560,19 @@
         drain(wdr.at[own, :], 22)
 
     drain(pr.at[main, :], 15)
-    drain(pr.at[down, :], 28)
     drain(rr.at[0:3, 0:32], 17)
-    drain(rr.at[0:3, 32:48], 27)
     drain(ym.at[0:15], 18)
-    drain(yd.at[0:15], 19)
-    drain(yd.at[0:16], 20)
+
+    @pl.when(c == 0)
+    def _():
+        drain(pr.at[down, :], 28)
+
+    @pl.when(c == 1)
+    def _():
+        drain(rr.at[0:3, 32:64], 27)
+        drain(yd.at[0:15], 19)
+        lend_down.wait_send()
+
     drain(ro.at[0:64, :], 24)
     got(ro.at[0:64, :], s_or)
 
@@ -573,19 +611,20 @@
             vmem((5 * BLK, BLK), F32),
             vmem((128, HALF), BF16),
             vmem((384, 512), F32),
-            vmem((192, 512), BF16),
-            vmem((192, 512), BF16),
-            vmem((4, 48, 512), BF16),
-            vmem((4, 48, 512), BF16),
+            vmem((256, 512), BF16),
+            vmem((256, 512), BF16),
+            vmem((4, 64, 512), BF16),
+            vmem((4, 64, 512), BF16),
             vmem((16, 32, 512), BF16),
-            vmem((32, 16, 512), BF16),
+            vmem((16, 32, 512), BF16),
             vmem((512, 512), BF16),
             vmem((512, 512), BF16),
-            vmem((192, 512), F32),
+            vmem((256, 512), F32),
             vmem((2, 512, 512), BF16),
             vmem((512, 512), BF16),
             vmem((128, HALF), BF16),
             vmem((8, HALF), F32),
+            vmem((512, HALF), BF16),
             dma((9,)),
             dma((2, 2)),
             dma((3,)),

time: 52.8 us -> 51.1 us (0.968)
  Pallas kernels: 52.1 us -> 50.4 us
    pallas_call x1, Pallas kernels: 51.3 us -> 49.6 us  [per_device(): pl.pallas_call(kernel, out_shape=(out, out), in_specs=[any_spec] * 9, out...]
where the time goes in v3:
time: 51.1 us; the launch traced here: 51 us
  Pallas kernels  50.4 us (99%)
  between operations  0.64 us (1%)
    pallas_call x1, Pallas kernels, per_device(): pl.pallas_call(kernel, out_shape=(out, out), in_specs=[any_spec] * 9, out...  49.6 us

profile of v3, /device:TPU:1, one launch (start us, length us, event | category | flops | bytes accessed | tf_op | source)
XLA Modules:
  0.0 51.0 jit_solution(331419014088583623)
XLA Ops:
  0.6 49.6 %plane.1 = (bf16[64,2048]{1,0:T(8,128)(2,1)S(1)}, bf16[64,2048]{1,0:T(8,128)(2,1)S(1)}) custom-call(bf16[64,2048]{1,0:T(8,128)(2,1)} %q_in.1, bf16[64,2048]{1,0:T(8,128)(2,1)} %k_in.1, bf16[64,2048]{1,0:T(8,128)(2,1)} %v_in.1, bf16[64,1024]{1,0:T(8,128)(2,1)} %ck_in.1, bf16[64,1024]{1,0:T(8,128)(2,1)} %cv_in.1, bf16[2,512,512]{2,1,0:T(8,128)(2,1)} %g_in.1, ...), custom_call_target="tpu_custom_call" | custom-call | tf_op jit(solution)/shard_map/plane/pallas_call | solution.py:594
  50.2 0.8 %write_out.1 = (bf16[64,2048]{1,0:T(8,128)(2,1)}, bf16[64,2048]{1,0:T(8,128)(2,1)}) custom-call(bf16[64,2048]{1,0:T(8,128)(2,1)S(1)} %get-tuple-element.4.att, bf16[64,2048]{1,0:T(8,128)(2,1)S(1)} %get-tuple-element.5.rec), custom_call_target="tpu_custom_call" | custom-call | tf_op jit(solution)/shard_map/write_out/pallas_call | solution.py:656

commit v4 on v3

--- a/solution.py
+++ b/solution.py
@@ -49,7 +49,7 @@
     q_in, k_in, v_in, ck_in, cv_in, g_in, l_in, d_in, r_in,
     att, rec,
     kf, vf, qf, kp, vp, wm, wq, wdq, wdr, wdt, kt, sc, ao, gd, ps, pr, gs, rr, ym, yd, xs, zs, ls,
-    fr, fd, ro, rt, hq,
+    fr, fd, ro, rt, hq, ql,
     s_loc, s_hp, s_par, s_ring, s_fwd, s_wy, s_wp, s_wr, s_wf, s_qr, s_qfw, s_rsp, s_rs, s_ag, s_ag2,
     s_dag, s_dag2, s_dp, s_fr, s_oa, s_or, snd,
 ):
@@ -455,9 +455,13 @@
         for index in range(2):
             got(wm.at[at(far * 128 + index * 64, 64), :], s_wf.at[index])
 
-    fr[c] = fresh(wm[...], xs[...])
-    lend = remote(fr.at[c], fr.at[c], snd.at[13], s_fr, partner)
-    lend.start()
+    lends = []
+    for index in range(2):
+        rows = slice(index * 256, index * 256 + 256)
+        fr[c, rows, :] = fresh(wm[rows, :], xs[rows, :])
+        part = fr.at[c, rows, :]
+        lends.append(remote(part, part, snd.at[13 + 16 * index], s_fr.at[index], partner))
+        lends[index].start()
 
     @pl.when(jnp.logical_not(source))
     def _():
@@ -483,13 +487,13 @@
 
     for way in range(2):
         got(qf.at[at(far * 128, 128), way * 512 : way * 512 + 512], s_qfw.at[way])
-    got(fr.at[p], s_fr)
-
-    def hide(block):
+    def lent():
+        for index in range(2):
+            got(fr.at[p, index * 256 : index * 256 + 256, :], s_fr.at[index])
+
+    def hide(block, query_lift):
         span = slice(block * BLK, (block + 1) * BLK)
-        asked = qf[:, span]
-        query_gate = dot(fr[0], asked)
-        query_lift = dot(fr[1], asked)
+        query_gate = dot(fr[0], qf[:, span])
         return (query_gate / (1.0 + jnp.exp(-query_gate)) * query_lift).astype(BF16)
 
     def settle(block, hidden):
@@ -501,8 +505,10 @@
 
     @pl.when(c == 0)
     def _():
+        lent()
         for block in range(NBLK):
-            hq[:, block * BLK : (block + 1) * BLK] = hide(block)
+            span = slice(block * BLK, (block + 1) * BLK)
+            hq[:, span] = hide(block, dot(fr[1], qf[:, span]))
         got(wdt, s_dp)
         for block in range(NBLK):
             settle(block, hq[:, block * BLK : (block + 1) * BLK])
@@ -510,7 +516,11 @@
     @pl.when(c == 1)
     def _():
         for block in range(NBLK):
-            settle(block, hide(block))
+            span = slice(block * BLK, (block + 1) * BLK)
+            ql[:, span] = dot(fr[1], qf[:, span])
+        lent()
+        for block in range(NBLK):
+            settle(block, hide(block, ql[:, block * BLK : (block + 1) * BLK]))
 
     def drain(ref, index):
         remote(ref, ref, snd.at[index], s_or, partner).wait_send()
@@ -521,7 +531,8 @@
     local(ao.at[own, :], att.at[:, half], s_loc.at[4]).wait()
     give.wait_send()
     got(ao.at[own, :], s_oa)
-    lend.wait_send()
+    for copy in lends:
+        copy.wait_send()
     for copy in share:
         copy.wait_send()
 
@@ -625,6 +636,7 @@
             vmem((128, HALF), BF16),
             vmem((8, HALF), F32),
             vmem((512, HALF), BF16),
+            vmem((512, HALF), F32),
             dma((9,)),
             dma((2, 2)),
             dma((3,)),
@@ -643,10 +655,10 @@
             dma((2, 4)),
             dma(()),
             dma(()),
+            dma((2,)),
             dma(()),
             dma(()),
-            dma(()),
-            dma((29,)),
+            dma((30,)),
         ],
         compiler_params=pltpu.CompilerParams(
             collective_id=0, has_side_effects=True, vmem_limit_bytes=48000000

time: 51.1 us -> 50.8 us (level)
  no operation moved by 1% of the time
where the time goes in v4:
time: 50.8 us
  Pallas kernels  50.1 us (99%)
  between operations  0.64 us (1%)
    pallas_call x1, Pallas kernels, per_device(): pl.pallas_call(kernel, out_shape=(out, out), in_specs=[any_spec] * 9, out...  49.3 us

profile of v4, /device:TPU:1, one launch (start us, length us, event | category | flops | bytes accessed | tf_op | source)
XLA Modules:
  0.0 50.8 jit_solution(1846955524156679754)
XLA Ops:
  0.6 49.3 %plane.1 = (bf16[64,2048]{1,0:T(8,128)(2,1)S(1)}, bf16[64,2048]{1,0:T(8,128)(2,1)S(1)}) custom-call(bf16[64,2048]{1,0:T(8,128)(2,1)} %q_in.1, bf16[64,2048]{1,0:T(8,128)(2,1)} %k_in.1, bf16[64,2048]{1,0:T(8,128)(2,1)} %v_in.1, bf16[64,1024]{1,0:T(8,128)(2,1)} %ck_in.1, bf16[64,1024]{1,0:T(8,128)(2,1)} %cv_in.1, bf16[2,512,512]{2,1,0:T(8,128)(2,1)} %g_in.1, ...), custom_call_target="tpu_custom_call" | custom-call | tf_op jit(solution)/shard_map/plane/pallas_call | solution.py:605
  49.9 0.8 %write_out.1 = (bf16[64,2048]{1,0:T(8,128)(2,1)}, bf16[64,2048]{1,0:T(8,128)(2,1)}) custom-call(bf16[64,2048]{1,0:T(8,128)(2,1)S(1)} %get-tuple-element.4.att, bf16[64,2048]{1,0:T(8,128)(2,1)S(1)} %get-tuple-element.5.rec), custom_call_target="tpu_custom_call" | custom-call | tf_op jit(solution)/shard_map/write_out/pallas_call | solution.py:668

commit v5 on v4

--- a/solution.py
+++ b/solution.py
@@ -226,16 +226,8 @@
 
     for load in loads:
         load.wait()
-    for index, dst in enumerate((kp, vp)):
-        for core in range(2):
-            got(dst.at[core * 64 : (core + 1) * 64, :], s_hp.at[index, core])
     for index, dst in enumerate((kf, vf, qf)):
         got(dst.at[at((2 * x + p) * 64, 64), :], s_par.at[index])
-
-    for block in range(NBLK):
-        span = slice(block * BLK, (block + 1) * BLK)
-        kt[block * BLK : (block + 1) * BLK, :] = kp[:, span].T
-        kt[HALF + block * BLK : HALF + (block + 1) * BLK, :] = kf[quarter, span].T
 
     row_at = lax.broadcasted_iota(jnp.int32, (BLK, BLK), 0)
     col_at = lax.broadcasted_iota(jnp.int32, (BLK, BLK), 1)
@@ -266,8 +258,6 @@
             blend = blend + dot(held, raised.astype(BF16))
         ao[:, first : first + BLK] = (blend / total).astype(BF16)
 
-    attend(0)
-
     for core, (first, second) in enumerate(((g_in, l_in), (l_in, g_in))):
 
         @pl.when(source & (c == core))
@@ -314,7 +304,6 @@
         ps[down, :] = gd[256:384, :].astype(BF16)
         remote(ps.at[down, :], pr.at[down, :], snd.at[28], s_rsp.at[1], partner).start()
 
-    attend(1)
 
     def pair_and_send(index, span, first, size, low):
         got(pr.at[span, :], s_rsp.at[index])
@@ -350,6 +339,16 @@
     def _():
         pair_and_send(1, down, 256, 32, 32)
 
+    for index, dst in enumerate((kp, vp)):
+        for core in range(2):
+            got(dst.at[core * 64 : (core + 1) * 64, :], s_hp.at[index, core])
+    for block in range(NBLK):
+        span = slice(block * BLK, (block + 1) * BLK)
+        kt[block * BLK : (block + 1) * BLK, :] = kp[:, span].T
+        kt[HALF + block * BLK : HALF + (block + 1) * BLK, :] = kf[quarter, span].T
+
+    attend(0)
+    attend(1)
     attend(2)
     attend(3)
     local(ao.at[own, :], att.at[:, half], s_loc.at[4]).start()

time: 50.8 us -> 50.5 us (level)
  Pallas kernels: 50.1 us -> 49.4 us
    pallas_call x1, Pallas kernels: 49.3 us -> 48.5 us  [per_device(): pl.pallas_call(kernel, out_shape=(out, out), in_specs=[any_spec] * 9, out...]
where the time goes in v5:
time: 50.5 us; the launch traced here: 50 us
  Pallas kernels  49.4 us (98%)
  between operations  0.64 us (1%)
    pallas_call x1, Pallas kernels, per_device(): pl.pallas_call(kernel, out_shape=(out, out), in_specs=[any_spec] * 9, out...  48.5 us

profile of v5, /device:TPU:1, one launch (start us, length us, event | category | flops | bytes accessed | tf_op | source)
XLA Modules:
  0.0 50.0 jit_solution(7719161265480020703)
XLA Ops:
  0.6 48.5 %plane.1 = (bf16[64,2048]{1,0:T(8,128)(2,1)S(1)}, bf16[64,2048]{1,0:T(8,128)(2,1)S(1)}) custom-call(bf16[64,2048]{1,0:T(8,128)(2,1)} %q_in.1, bf16[64,2048]{1,0:T(8,128)(2,1)} %k_in.1, bf16[64,2048]{1,0:T(8,128)(2,1)} %v_in.1, bf16[64,1024]{1,0:T(8,128)(2,1)} %ck_in.1, bf16[64,1024]{1,0:T(8,128)(2,1)} %cv_in.1, bf16[2,512,512]{2,1,0:T(8,128)(2,1)} %g_in.1, ...), custom_call_target="tpu_custom_call" | custom-call | tf_op jit(solution)/shard_map/plane/pallas_call | solution.py:604
  49.2 0.8 %write_out.1 = (bf16[64,2048]{1,0:T(8,128)(2,1)}, bf16[64,2048]{1,0:T(8,128)(2,1)}) custom-call(bf16[64,2048]{1,0:T(8,128)(2,1)S(1)} %get-tuple-element.4.att, bf16[64,2048]{1,0:T(8,128)(2,1)S(1)} %get-tuple-element.5.rec), custom_call_target="tpu_custom_call" | custom-call | tf_op jit(solution)/shard_map/write_out/pallas_call | solution.py:667
